TPU v7x, 32 devices: a whole 2x2x4 slice. The times are simulated.
32 devices in a mesh: grp: 1, win: 32 (over z, y, x, core).
Axes of the slice: x: 2, y: 2, z: 4, core: 2. Of those that a mesh axis runs over, the one named last changes fastest.
Arguments:
- tokens: bfloat16 [2, 8, 64, 96, 384], P('grp', None, None, 'win'), may hold values from -6 to 6
- w_upper: bfloat16 [384, 640], replicated, may hold values from -0.3125 to 0.3125
- w_surface: bfloat16 [384, 256], replicated, may hold values from -0.3125 to 0.3125
- bias: float32 [69], replicated, may hold values from -1 to 1
Outputs:
- fields: bfloat16 [2, 17664, 384], P('grp', 'win')
All inputs are finite; a program needn't handle non-finite values.
Results may differ from a plain program's by a relative error of at most 0.0048.
Values may be sent and summed in bfloat16 or wider, within the bound.
A program may use at most 128 MiB of HBM per device.

v0:
```python
import jax
import jax.numpy as jnp
from jax import lax
from jax.sharding import PartitionSpec as P

VARS_UP = 5
LEVELS = 13
VARS_SF = 4
PATCH = 4


def intersection_add(values, axis):
    first = lax.index_in_dim(values, 0, axis + 1, keepdims=False)
    second = lax.index_in_dim(values, 1, axis + 1, keepdims=False)
    pad_first = [(0, 0)] * first.ndim
    pad_second = [(0, 0)] * first.ndim
    pad_first[axis] = (0, 1)
    pad_second[axis] = (1, 0)
    return jnp.pad(first, pad_first) + jnp.pad(second, pad_second)


def latitude_add(values):
    first = values[..., 0, :, :]
    second = values[..., 1, :, :]
    pad_first = [(0, 0)] * (first.ndim - 1) + [(0, 1)]
    pad_second = [(0, 0)] * (first.ndim - 1) + [(1, 0)]
    summed = jnp.pad(first, pad_first) + jnp.pad(second, pad_second)
    return jnp.swapaxes(summed, -1, -2)


def project(tokens, w_upper, w_surface):
    members, tok_levels, lat_rows, lon_cols, width = tokens.shape
    upper_levels = tok_levels - 1
    rim_width = PATCH // 2
    frame_width = (lon_cols + 1) * PATCH
    upper_tok = jnp.transpose(tokens[:, :upper_levels], (0, 1, 3, 4, 2))
    kernel_up = w_upper.reshape(width, VARS_UP, 2, 2, PATCH, 2, PATCH)
    upper = jnp.einsum(
        "dvlpqrs,mzjdi->vlpqrsmzji", kernel_up, upper_tok, preferred_element_type=jnp.float32
    )
    upper = jnp.transpose(upper, (6, 8, 4, 5, 0, 7, 1, 2, 3, 9))
    upper = intersection_add(upper, 1)
    upper = latitude_add(upper)
    upper = upper.reshape(members, frame_width, VARS_UP, 2 * upper_levels, (lat_rows + 1) * PATCH)
    upper = upper[:, :, :, :LEVELS, rim_width : rim_width + lat_rows * PATCH]
    upper = upper.reshape(members, frame_width, VARS_UP * LEVELS, lat_rows * PATCH)
    surface_tok = jnp.transpose(tokens[:, upper_levels], (0, 2, 3, 1))
    kernel_sf = w_surface.reshape(width, VARS_SF, 2, PATCH, 2, PATCH)
    surface = jnp.einsum(
        "dvpqrs,mjdi->vpqrsmji", kernel_sf, surface_tok, preferred_element_type=jnp.float32
    )
    surface = jnp.transpose(surface, (5, 6, 3, 4, 0, 1, 2, 7))
    surface = intersection_add(surface, 1)
    surface = latitude_add(surface)
    surface = surface.reshape(members, frame_width, VARS_SF, (lat_rows + 1) * PATCH)
    surface = surface[:, :, :, rim_width : rim_width + lat_rows * PATCH]
    joined = jnp.concatenate([upper, surface], axis=2).astype(jnp.bfloat16)
    return joined.reshape(members, frame_width, -1)


def deliver(frames, bias, lat_rows):
    rim_width = PATCH // 2
    members, frame_width, all_rows = frames.shape
    columns = frame_width - 2 * rim_width
    windows = lax.axis_size("win")
    received = lax.all_to_all(frames, "win", split_axis=2, concat_axis=1, tiled=True)
    own_rows = received.shape[2]
    received = received.reshape(members, windows, frame_width, own_rows)
    inner = received[:, :, rim_width : frame_width - rim_width, :].astype(jnp.float32)
    from_left = jnp.roll(received[:, :, frame_width - rim_width :, :], 1, axis=1).astype(
        jnp.float32
    )
    from_right = jnp.roll(received[:, :, :rim_width, :], -1, axis=1).astype(jnp.float32)
    summed = inner + jnp.pad(from_left, ((0, 0), (0, 0), (0, columns - rim_width), (0, 0)))
    summed = summed + jnp.pad(from_right, ((0, 0), (0, 0), (columns - rim_width, 0), (0, 0)))
    first_row = lax.axis_index("win") * own_rows
    row_ids = first_row + jnp.arange(own_rows, dtype=jnp.int32)
    channel = row_ids // (lat_rows * PATCH)
    selector = (channel[:, None] == jnp.arange(bias.shape[0], dtype=jnp.int32)[None, :]).astype(
        jnp.float32
    )
    bias_rows = jnp.dot(selector, bias, precision=lax.Precision.HIGHEST)
    image = (summed + bias_rows[None, None, None, :]).astype(jnp.bfloat16)
    image = image.reshape(members, windows * columns, own_rows)
    return jnp.transpose(image, (0, 2, 1))


def body(tokens, w_upper, w_surface, bias):
    lat_rows = tokens.shape[2]
    frames = project(tokens, w_upper, w_surface)
    return deliver(frames, bias, lat_rows)


def solution(mesh):
    placed = (P("grp", None, None, "win", None), P(), P(), P())
    return jax.shard_map(
        body, mesh=mesh, in_specs=placed, out_specs=P("grp", "win", None), check_vma=False
    )
```

profile of v0, /device:TPU:0, one launch (start us, length us, event | category | flops | bytes accessed | tf_op | source)
XLA Modules:
  0.0 201.6 jit_solution(15619941665332143231)
XLA Ops:
  0.0 1.3 copy.25
  1.4 7.7 %convolution_bitcast_fusion = f32[2,3,2,4,5,7,2,2,4,64]{9,4,1,5,0,3,2,8,7,6:T(8,128)S(1)} fusion(bf16[2,8,64,3,384]{4,2,3,1,0:T(8,128)(2,1)} %param.4, bf16[384,5,2,2,4,2,4,1,1,1]{0,6,5,4,3,2,1,9,8,7:T(4,128)(2,1)S(1)} %bitcast.81), kind=kOutput, calls=%fused_computation.4 | convolution fusion | flops 1321205760 | bytes 9437184 | tf_op jit(solution)/shard_map/dvlpqrs,mzjdi->vlpqrsmzji/dot_general | solution.py:38
  9.1 8.7 %slice_bitcast_fusion.1 = (f32[2,3,4,5,7,2,2,4,64]{8,3,1,4,0,2,7,6,5:T(8,128)}, f32[2,3,4,5,7,2,2,4,64]{8,3,1,4,0,2,7,6,5:T(8,128)}) fusion(f32[2,3,2,4,5,7,2,2,4,64]{9,4,1,5,0,3,2,8,7,6:T(8,128)S(1)} %convolution_bitcast_fusion), kind=kLoop, calls=%fused_computation.3 | loop fusion | bytes 13762560 | tf_op jit(solution)/shard_map/squeeze | solution.py:13
  17.8 12.0 %fusion.1 = (f32[2,4,4,5,7,2,4,64]{7,3,1,4,0,2,6,5:T(8,128)S(1)}, f32[2,4,4,5,7,2,4,64]{7,3,1,4,0,2,6,5:T(8,128)}) fusion(f32[2,3,4,5,7,2,2,4,64]{8,3,1,4,0,2,7,6,5:T(8,128)} %get-tuple-element.7, f32[2,3,4,5,7,2,2,4,64]{8,3,1,4,0,2,7,6,5:T(8,128)} %get-tuple-element.8), kind=kLoop, calls=%fused_computation.6 | loop fusion | flops 1146880 | bytes 11468800 | tf_op jit(solution)/shard_map/squeeze | solution.py:23
  29.9 6.9 %fusion.3 = bf16[2,4,4,5,7,2,65,4]{6,3,1,4,0,2,7,5:T(8,128)(2,1)} fusion(f32[2,4,4,5,7,2,4,64]{7,3,1,4,0,2,6,5:T(8,128)} %get-tuple-element.6, f32[2,4,4,5,7,2,4,64]{7,3,1,4,0,2,6,5:T(8,128)S(1)} %get-tuple-element.5), kind=kLoop, calls=%fused_computation.10 | loop fusion | flops 1164800 | bytes 5752320 | tf_op jit(solution)/shard_map/transpose | solution.py:28
  36.7 31.0 %copy.29 = bf16[2,4,4,5,7,2,65,4]{7,6,2,1,5,4,3,0:T(8,128)(2,1)} copy(bf16[2,4,4,5,7,2,65,4]{6,3,1,4,0,2,7,5:T(8,128)(2,1)} %fusion.3) | data formatting | bytes 2329600 | tf_op jit(solution)/shard_map/transpose | solution.py:28
  67.7 39.4 %reshape.47 = bf16[2,16,5,14,260]{4,1,3,2,0:T(8,128)(2,1)S(1)} reshape(bf16[2,4,4,5,7,2,65,4]{7,6,2,1,5,4,3,0:T(8,128)(2,1)} %copy.29) | data formatting | bytes 2329600 | tf_op jit(solution)/shard_map/reshape | solution.py:44
  107.0 0.5 slice.84
  107.5 0.2 copy.30
  107.8 1.4 convolution_bitcast_fusion.1
  109.3 0.2 fusion.16
  109.5 0.9 fusion.20
  110.4 2.0 %copy.34 = bf16[2,4,4,4,65,4]{5,4,2,1,3,0:T(8,128)(2,1)S(1)} copy(bf16[2,4,4,4,65,4]{4,2,1,0,5,3:T(4,128)(2,1)} %fusion.20) | data formatting | bytes 133120 | tf_op jit(solution)/shard_map/transpose | solution.py:28
  112.4 1.3 reshape.50
  113.9 13.7 %copy.46 = bf16[2,16,69,256]{1,0,3,2:T(2,128)(2,1)} copy(bf16[2,16,69,256]{3,1,2,0:T(8,128)(2,1)S(1)} %pad_maximum_fusion) | data formatting | bytes 2260992 | tf_op jit(solution)/shard_map/convert_element_type | solution.py:57
  127.6 11.7 %reshape.60 = bf16[32,2,8832]{2,1,0:T(2,128)(2,1)} reshape(bf16[17664,2,16]{2,1,0:T(2,128)(2,1)} %bitcast.74) | data formatting | bytes 2260992
  139.4 7.3 %all-to-all-start = ((bf16[32,2,8832]{2,1,0:T(2,128)(2,1)}), bf16[32,2,8832]{2,1,0:T(2,128)(2,1)S(1)}, u32[]{:S(2)}, u32[]{:S(2)}) async-start(bf16[32,2,8832]{2,1,0:T(2,128)(2,1)} %reshape.60), calls=%async_computation | async-start | bytes 2260992 | tf_op jit(solution)/shard_map/all_to_all | solution.py:66
  146.7 0.3 convolution_reduce_fusion
  147.1 27.6 %all-to-all-done = bf16[32,2,8832]{2,1,0:T(2,128)(2,1)S(1)} async-done(((bf16[32,2,8832]{2,1,0:T(2,128)(2,1)}), bf16[32,2,8832]{2,1,0:T(2,128)(2,1)S(1)}, u32[]{:S(2)}, u32[]{:S(2)}) %all-to-all-start) | async-done | bytes 1130528 | tf_op jit(solution)/shard_map/all_to_all | solution.py:66
  174.7 8.2 %reshape.61 = bf16[17664,2,16]{2,1,0:T(2,128)(2,1)} reshape(bf16[32,2,8832]{2,1,0:T(2,128)(2,1)S(1)} %all-to-all-done) | data formatting | bytes 2260992
  182.9 14.4 %copy.47 = bf16[2,16,32,552]{3,2,1,0:T(8,128)(2,1)S(1)} copy(bf16[2,16,32,552]{1,0,3,2:T(2,128)(2,1)} %bitcast.75) | data formatting | bytes 2260992 | tf_op jit(solution)/shard_map/all_to_all | solution.py:66
  197.4 0.3 add_convert_fusion.1
  197.7 1.0 copy.38
  198.7 2.9 %copy.39 = bf16[2,552,384]{2,1,0:T(8,128)(2,1)} copy(bf16[2,552,384]{1,0,2:T(2,128)(2,1)S(1)} %bitcast.80) | data formatting | bytes 1695744 | tf_op jit(solution)/shard_map/transpose | solution.py:85
  (12 shorter events, 0.6 us)
Async XLA Ops:
  0.0 146.7 %copy-start = (f32[69]{0:T(128)S(1)}, f32[69]{0:T(128)}, u32[]{:S(2)}) copy-start(f32[69]{0:T(128)} %param.7) | copy-start | bytes 832
  67.7 39.8 %copy-start.1 = (bf16[384,256]{1,0:T(8,128)(2,1)S(1)}, bf16[384,256]{1,0:T(8,128)(2,1)}, u32[]{:S(2)}) copy-start(bf16[384,256]{1,0:T(8,128)(2,1)} %param.6) | copy-start | bytes 589828
  139.4 35.3 %all-to-all-start = ((bf16[32,2,8832]{2,1,0:T(2,128)(2,1)}), bf16[32,2,8832]{2,1,0:T(2,128)(2,1)S(1)}, u32[]{:S(2)}, u32[]{:S(2)}) async-start(bf16[32,2,8832]{2,1,0:T(2,128)(2,1)} %reshape.60), calls=%async_computation | async-start | bytes 2260992 | tf_op jit(solution)/shard_map/all_to_all | solution.py:66
where the time goes:
time: 204 us; the launch traced here: 202 us
  local copies, waits for them, and re-layouts  137 us (67%)
  waiting for transfers between devices  27.6 us (14%)
  other arithmetic  20.3 us (10%)
  matrix products  9.46 us (5%)
  starting transfers between devices  7.33 us (4%)
    reshape x1, local copies, waits for them, and re-layouts, project(): upper.reshape(members, frame_width, VARS_UP, 2 * upper_levels, (lat_rows...  39.4 us
    transpose x2, local copies, waits for them, and re-layouts, latitude_add(): return jnp.swapaxes(summed, -1, -2)  33 us
    all_to_all x1, waiting for transfers between devices, deliver(): lax.all_to_all(frames, 'win', split_axis=2, concat_axis=1, tiled=True)  27.6 us
    unnamed x8, local copies, waits for them, and re-layouts  21.4 us
    all_to_all x1, local copies, waits for them, and re-layouts, deliver(): lax.all_to_all(frames, 'win', split_axis=2, concat_axis=1, tiled=True)  14.4 us
    convert_element_type x1, local copies, waits for them, and re-layouts, project(): joined = jnp.concatenate([upper, surface], axis=2).astype(jnp.bfloat16)  13.7 us
    squeeze x2, other arithmetic, latitude_add(): first = values[..., 0, :, :]  12.2 us
    squeeze x2, local copies, waits for them, and re-layouts, intersection_add(): first = lax.index_in_dim(values, 0, axis + 1, keepdims=False)  8.84 us
  transfers between devices with their start and end apart: 1, of which 1 were waited for; matrix products, arithmetic and copies ran while one was open for 0% of the time, Pallas kernels for 0%

commit v1 on v0

--- a/solution.py
+++ b/solution.py
@@ -63,7 +63,9 @@
     members, frame_width, all_rows = frames.shape
     columns = frame_width - 2 * rim_width
     windows = lax.axis_size("win")
-    received = lax.all_to_all(frames, "win", split_axis=2, concat_axis=1, tiled=True)
+    pieces = jnp.split(frames, lax.axis_size("win"), axis=2)
+    incoming = lax.all_to_all(jnp.stack(pieces), "win", 0, 0)
+    received = jnp.concatenate(incoming, axis=1)
     own_rows = received.shape[2]
     received = received.reshape(members, windows, frame_width, own_rows)
     inner = received[:, :, rim_width : frame_width - rim_width, :].astype(jnp.float32)

time: 204 us -> 185 us (0.907)
  local copies, waits for them, and re-layouts: 137 us -> 114 us
  waiting for transfers between devices: 27.6 us -> 31.6 us
    all_to_all x1 -> x0, local copies, waits for them, and re-layouts: 14.4 us -> none  [deliver(): lax.all_to_all(frames, 'win', split_axis=2, concat_axis=1, tiled=True)]
    convert_element_type x1, local copies, waits for them, and re-layouts: 13.7 us -> 0.65 us  [project(): joined = jnp.concatenate([upper, surface], axis=2).astype(jnp.bfloat16)]
    all_to_all x1, waiting for transfers between devices: 27.6 us -> 31.6 us  [deliver(): incoming = lax.all_to_all(jnp.stack(pieces), 'win', 0, 0)]
    unnamed x8 -> x37, local copies, waits for them, and re-layouts: 21.4 us -> 23.4 us
where the time goes in v1:
time: 185 us; the launch traced here: 183 us
  local copies, waits for them, and re-layouts  114 us (62%)
  waiting for transfers between devices  31.6 us (17%)
  other arithmetic  21.1 us (11%)
  matrix products  9.46 us (5%)
  starting transfers between devices  7.33 us (4%)
    reshape x1, local copies, waits for them, and re-layouts, project(): upper.reshape(members, frame_width, VARS_UP, 2 * upper_levels, (lat_rows...  39.3 us
    transpose x2, local copies, waits for them, and re-layouts, latitude_add(): return jnp.swapaxes(summed, -1, -2)  33 us
    all_to_all x1, waiting for transfers between devices, deliver(): incoming = lax.all_to_all(jnp.stack(pieces), 'win', 0, 0)  31.6 us
    unnamed x37, local copies, waits for them, and re-layouts  23.4 us
    squeeze x2, other arithmetic, latitude_add(): first = values[..., 0, :, :]  12.2 us
    squeeze x2, local copies, waits for them, and re-layouts, intersection_add(): first = lax.index_in_dim(values, 0, axis + 1, keepdims=False)  8.84 us
    transpose x2, other arithmetic, latitude_add(): return jnp.swapaxes(summed, -1, -2)  7.72 us
    dot_general x1, matrix products, project(): jnp.einsum('dvlpqrs,mzjdi->vlpqrsmzji', kernel_up, upper_tok, preferred_e...  7.67 us
  transfers between devices with their start and end apart: 1, of which 1 were waited for; matrix products, arithmetic and copies ran while one was open for 0% of the time, Pallas kernels for 0%

profile of v1, /device:TPU:0, one launch (start us, length us, event | category | flops | bytes accessed | tf_op | source)
XLA Modules:
  0.0 183.3 jit_solution(2037318045292900410)
XLA Ops:
  0.0 1.3 copy.56
  1.4 7.7 %convolution_bitcast_fusion = f32[2,3,2,4,5,7,2,2,4,64]{9,4,1,5,0,3,2,8,7,6:T(8,128)S(1)} fusion(bf16[2,8,64,3,384]{4,2,3,1,0:T(8,128)(2,1)} %param.4, bf16[384,5,2,2,4,2,4,1,1,1]{0,6,5,4,3,2,1,9,8,7:T(4,128)(2,1)S(1)} %bitcast.203), kind=kOutput, calls=%fused_computation.4 | convolution fusion | flops 1321205760 | bytes 9437184 | tf_op jit(solution)/shard_map/dvlpqrs,mzjdi->vlpqrsmzji/dot_general | solution.py:38
  9.1 8.7 %slice_bitcast_fusion.1 = (f32[2,3,4,5,7,2,2,4,64]{8,3,1,4,0,2,7,6,5:T(8,128)}, f32[2,3,4,5,7,2,2,4,64]{8,3,1,4,0,2,7,6,5:T(8,128)}) fusion(f32[2,3,2,4,5,7,2,2,4,64]{9,4,1,5,0,3,2,8,7,6:T(8,128)S(1)} %convolution_bitcast_fusion), kind=kLoop, calls=%fused_computation.3 | loop fusion | bytes 13762560 | tf_op jit(solution)/shard_map/squeeze | solution.py:13
  17.8 12.0 %fusion.1 = (f32[2,4,4,5,7,2,4,64]{7,3,1,4,0,2,6,5:T(8,128)S(1)}, f32[2,4,4,5,7,2,4,64]{7,3,1,4,0,2,6,5:T(8,128)}) fusion(f32[2,3,4,5,7,2,2,4,64]{8,3,1,4,0,2,7,6,5:T(8,128)} %get-tuple-element.7, f32[2,3,4,5,7,2,2,4,64]{8,3,1,4,0,2,7,6,5:T(8,128)} %get-tuple-element.8), kind=kLoop, calls=%fused_computation.6 | loop fusion | flops 1146880 | bytes 11468800 | tf_op jit(solution)/shard_map/squeeze | solution.py:23
  29.9 6.9 %fusion.3 = bf16[2,4,4,5,7,2,65,4]{6,3,1,4,0,2,7,5:T(8,128)(2,1)} fusion(f32[2,4,4,5,7,2,4,64]{7,3,1,4,0,2,6,5:T(8,128)} %get-tuple-element.6, f32[2,4,4,5,7,2,4,64]{7,3,1,4,0,2,6,5:T(8,128)S(1)} %get-tuple-element.5), kind=kLoop, calls=%fused_computation.10 | loop fusion | flops 1164800 | bytes 5752320 | tf_op jit(solution)/shard_map/transpose | solution.py:28
  36.7 31.0 %copy.60 = bf16[2,4,4,5,7,2,65,4]{7,6,2,1,5,4,3,0:T(8,128)(2,1)} copy(bf16[2,4,4,5,7,2,65,4]{6,3,1,4,0,2,7,5:T(8,128)(2,1)} %fusion.3) | data formatting | bytes 2329600 | tf_op jit(solution)/shard_map/transpose | solution.py:28
  67.7 39.3 %reshape.48 = bf16[2,16,5,14,260]{4,1,3,2,0:T(8,128)(2,1)S(1)} reshape(bf16[2,4,4,5,7,2,65,4]{7,6,2,1,5,4,3,0:T(8,128)(2,1)} %copy.60) | data formatting | bytes 2329600 | tf_op jit(solution)/shard_map/reshape | solution.py:44
  108.6 1.4 convolution_bitcast_fusion.1
  110.4 0.9 fusion.20
  111.3 2.0 %copy.65 = bf16[2,4,4,4,65,4]{5,4,2,1,3,0:T(8,128)(2,1)S(1)} copy(bf16[2,4,4,4,65,4]{4,2,1,0,5,3:T(4,128)(2,1)} %fusion.20) | data formatting | bytes 133120 | tf_op jit(solution)/shard_map/transpose | solution.py:28
  113.3 1.9 %reshape.51 = bf16[2,16,4,260]{3,1,2,0:T(8,128)(2,1)} reshape(bf16[2,4,4,4,65,4]{5,4,2,1,3,0:T(8,128)(2,1)S(1)} %copy.65) | data formatting | bytes 133120 | tf_op jit(solution)/shard_map/reshape | solution.py:55
  115.2 1.0 slice.89
  117.6 0.7 constant_dynamic-update-slice_fusion.30
  124.5 0.7 constant_dynamic-update-slice_fusion.20
  126.6 0.7 constant_dynamic-update-slice_fusion.17
  128.6 0.7 constant_dynamic-update-slice_fusion.14
  130.0 0.7 constant_dynamic-update-slice_fusion.12
  134.2 0.7 constant_dynamic-update-slice_fusion.6
  136.3 0.7 constant_dynamic-update-slice_fusion.3
  139.0 7.3 %all-to-all-start = ((bf16[32,2,16,552]{3,2,1,0:T(8,128)(2,1)}), bf16[32,2,16,552]{3,2,1,0:T(8,128)(2,1)S(1)}, u32[]{:S(2)}, u32[]{:S(2)}) async-start(bf16[32,2,16,552]{3,2,1,0:T(8,128)(2,1)} %constant_dynamic-update-slice_fusion), calls=%async_computation | async-start | bytes 2621440 | tf_op jit(solution)/shard_map/all_to_all | solution.py:67
  146.8 31.6 %all-to-all-done = bf16[32,2,16,552]{3,2,1,0:T(8,128)(2,1)S(1)} async-done(((bf16[32,2,16,552]{3,2,1,0:T(8,128)(2,1)}), bf16[32,2,16,552]{3,2,1,0:T(8,128)(2,1)S(1)}, u32[]{:S(2)}, u32[]{:S(2)}) %all-to-all-start) | async-done | bytes 1130528 | tf_op jit(solution)/shard_map/all_to_all | solution.py:67
  178.6 1.0 add_convert_fusion.1
  179.6 0.8 copy.68
  180.4 2.9 %copy.69 = bf16[2,552,384]{2,1,0:T(8,128)(2,1)} copy(bf16[2,552,384]{1,0,2:T(2,128)(2,1)S(1)} %bitcast.202) | data formatting | bytes 1695744 | tf_op jit(solution)/shard_map/transpose | solution.py:87
  (43 shorter events, 20.6 us)
Async XLA Ops:
  0.0 146.4 %copy-start = (f32[69]{0:T(128)S(1)}, f32[69]{0:T(128)}, u32[]{:S(2)}) copy-start(f32[69]{0:T(128)} %param.7) | copy-start | bytes 832
  107.5 0.9 copy-start.1
  139.0 39.3 %all-to-all-start = ((bf16[32,2,16,552]{3,2,1,0:T(8,128)(2,1)}), bf16[32,2,16,552]{3,2,1,0:T(8,128)(2,1)S(1)}, u32[]{:S(2)}, u32[]{:S(2)}) async-start(bf16[32,2,16,552]{3,2,1,0:T(8,128)(2,1)} %constant_dynamic-update-slice_fusion), calls=%async_computation | async-start | bytes 2621440 | tf_op jit(solution)/shard_map/all_to_all | solution.py:67
